TPU v7x, 256 devices: a whole 4x4x8 slice. The times are simulated.
256 devices in a mesh: row: 32 (over y, x, core), col: 8 (over z).
Axes of the slice: x: 4, y: 4, z: 8, core: 2. Of those that a mesh axis runs over, the one named last changes fastest.
Arguments:
- vectors_window: float32 [32, 32, 64, 1024], P(None, 'row', None, 'col'), may hold values from -6 to 6
- column_strip: float32 [32, 32, 64, 1024], P(None, 'row', None, 'col'), may hold values from -6 to 6
- row_strip: float32 [1024, 64, 8, 128], P('row', None, 'col'), may hold values from -6 to 6
- factor: float32 [1024, 1024], P('row', 'col'), may hold values from -2 to 2
- window_start: int32 [1], replicated, may hold values from 1 to 64512
- deflated: int32 [1], replicated, may hold values from 0 to 512
Outputs:
- vectors_updated: float32 [32, 32, 64, 1024], P(None, 'row', None, 'col')
- column_updated: float32 [32, 32, 64, 1024], P(None, 'row', None, 'col')
- row_updated: float32 [1024, 64, 8, 128], P('row', None, 'col')
All inputs are finite; a program needn't handle non-finite values.
Results may differ from a plain program's by a relative error of at most 0.0003.
Values sent between devices are 32-bit elements; how exact they have to be, the bound alone decides.
A program may use at most 64 MiB of HBM per device.

v0:
```python
import jax
import jax.numpy as jnp
from jax import lax
from jax.sharding import PartitionSpec as P

W = 1024


def from_everyone(x, axis):
    peers = lax.axis_size(axis)
    return lax.all_to_all(jnp.broadcast_to(x[None], (peers, *x.shape)), axis, 0, 0, tiled=True)


def laid_out(pieces, dim):
    dims = list(pieces.shape[1:])
    dims[dim] *= pieces.shape[0]
    return jnp.moveaxis(pieces, 0, dim).reshape(dims)


def gather_directly(x, axis, dim):
    pieces = from_everyone(x, axis)
    return laid_out(pieces, dim)


def reflect(factor, deflated):
    columns = jnp.arange(W, dtype=jnp.int32)
    kept_count = W - deflated[0]
    spike_row = jnp.where(columns < kept_count, factor[0], 0.0)
    squares = jnp.sum(spike_row * spike_row)
    corner = factor[0, 0]
    magnitude = jnp.sqrt(squares + 1e-06)
    signum = jnp.where(corner >= 0, 1.0, -1.0)
    vector = spike_row + jnp.where(columns == 0, signum * magnitude, 0.0)
    denominator = squares + 2.0 * jnp.abs(corner) * magnitude + magnitude * magnitude
    scaling = 2.0 / denominator
    reflected_image = jnp.dot(factor, vector, precision=lax.Precision.HIGHEST)
    return factor - scaling * reflected_image[:, None] * vector[None, :]


def body(vectors_window, column_strip, row_strip, factor, window_start, deflated):
    highest = lax.Precision.HIGHEST
    row_position = lax.axis_index("row")
    column_position = lax.axis_index("col")
    start_row = window_start[0]
    widened = gather_directly(factor, "col", 1)
    rotation = reflect(lax.all_gather(widened, "row", axis=0, tiled=True), deflated)
    rounds = vectors_window.shape[0]
    blocks = vectors_window.shape[2]
    local_width = vectors_window.shape[3]
    z_blocks = vectors_window.reshape(rounds, blocks, local_width)
    strip_blocks = column_strip.reshape(rounds, blocks, local_width)
    z_turned = jnp.einsum(
        "rbk,kj->rbj",
        lax.all_to_all(z_blocks, "col", split_axis=1, concat_axis=2, tiled=True),
        rotation,
        precision=highest,
    )
    strip_turned = jnp.einsum(
        "rbk,kj->rbj",
        lax.all_to_all(strip_blocks, "col", split_axis=1, concat_axis=2, tiled=True),
        rotation,
        precision=highest,
    )
    z_rotated = lax.all_to_all(z_turned, "col", split_axis=2, concat_axis=1, tiled=True)
    strip_rotated = lax.all_to_all(strip_turned, "col", split_axis=2, concat_axis=1, tiled=True)
    row_count = lax.axis_size("row")
    round_number = jnp.arange(rounds, dtype=jnp.int32)[:, None]
    block_number = jnp.arange(blocks, dtype=jnp.int32)[None, :]
    row_number = (round_number * row_count + row_position) * blocks + block_number
    column_updated = jnp.where(
        row_number[:, :, None] < start_row, strip_rotated, strip_blocks
    ).reshape(column_strip.shape)
    vectors_updated = z_rotated.reshape(vectors_window.shape)
    strip_rows = row_strip.shape[0]
    flat_strip = row_strip.reshape(strip_rows, -1)
    stacked = lax.all_to_all(flat_strip, "row", split_axis=1, concat_axis=0, tiled=True)
    rotated_rows = lax.dot_general(rotation, stacked, (((0,), (0,)), ((), ())), precision=highest)
    returned = lax.all_to_all(rotated_rows, "row", split_axis=0, concat_axis=1, tiled=True)
    column_count = lax.axis_size("col")
    column_rounds = row_strip.shape[1]
    column_block = row_strip.shape[3]
    round_index = jnp.arange(column_rounds, dtype=jnp.int32)[:, None]
    lane_index = jnp.arange(column_block, dtype=jnp.int32)[None, :]
    column_number = (round_index * column_count + column_position) * column_block + lane_index
    row_updated = jnp.where(
        column_number[None, :, None, :] >= start_row + W,
        returned.reshape(row_strip.shape),
        row_strip,
    )
    return (vectors_updated, column_updated, row_updated)


def solution(mesh):
    return jax.shard_map(
        body,
        mesh=mesh,
        in_specs=(
            P(None, "row", None, "col"),
            P(None, "row", None, "col"),
            P("row", None, "col", None),
            P("row", "col"),
            P(),
            P(),
        ),
        out_specs=(
            P(None, "row", None, "col"),
            P(None, "row", None, "col"),
            P("row", None, "col", None),
        ),
        check_vma=False,
    )
```

profile of v0, /device:TPU:1, one launch (start us, length us, event | category | flops | bytes accessed | tf_op | source)
XLA Modules:
  0.0 231.8 jit_solution(5835078651876137352)
XLA Ops:
  7.9 16.6 %all_to_all.106 = f32[8,32,128]{2,1,0:T(8,128)S(1)} all-to-all(f32[8,32,128]{2,1,0:T(8,128)S(1)} %broadcast_in_dim.44), channel_id=1, replica_groups=mesh['row'=32,'col'=8] {'col'}, dimensions={0} | all-to-all | bytes 262144 | tf_op jit(solution)/shard_map/all_to_all | solution.py:11
  25.7 4.4 %reduce.3 = f32[32,64,128]{2,1,0:T(8,128)S(1)} reduce(f32[32,64,1,128]{3,2,1,0:T(1,128)} %param.8, f32[]{:T(128)} %broadcast.101), dimensions={2}, to_apply=%param.8.reduce_sub_computation.3 | reduce | bytes 2097156 | tf_op args[2]
  32.0 9.4 %all-to-all-start.5 = ((f32[32,32,256]{2,0,1:T(8,128)}), f32[32,32,256]{2,0,1:T(8,128)S(1)}, u32[]{:S(2)}, u32[]{:S(2)}) async-start(f32[32,32,256]{2,0,1:T(8,128)} %copy.61), calls=%async_computation.5 | async-start | bytes 2097152 | tf_op jit(solution)/shard_map/all_to_all | solution.py:76
  41.4 2.8 %copy.74 = f32[32,1,64,128]{3,0,2,1:T(8,128)} copy(f32[32,1,64,128]{3,2,1,0:T(8,128)} %param.6) | data formatting | bytes 2097152 | tf_op args[0]
  44.2 14.1 %all-to-all-done.5 = f32[32,32,256]{2,0,1:T(8,128)S(1)} async-done(((f32[32,32,256]{2,0,1:T(8,128)}), f32[32,32,256]{2,0,1:T(8,128)S(1)}, u32[]{:S(2)}, u32[]{:S(2)}) %all-to-all-start.5) | async-done | bytes 1048608 | tf_op jit(solution)/shard_map/all_to_all | solution.py:76
  58.4 3.6 %all-to-all-start.1 = ((f32[32,64,128]{2,0,1:T(8,128)}), f32[32,64,128]{2,0,1:T(8,128)S(1)}, u32[]{:S(2)}, u32[]{:S(2)}) async-start(f32[32,64,128]{2,0,1:T(8,128)} %bitcast.78), calls=%async_computation.1 | async-start | bytes 2097152 | tf_op jit(solution)/shard_map/all_to_all | solution.py:54
  64.2 16.0 %all-gather.2.cloned.1.call-done = f32[1024,1024]{1,0:T(8,128)} async-done(((f32[32,1024]{1,0:T(8,128)}), f32[1024,1024]{1,0:T(8,128)}) %all-gather.2.cloned.1.call-update) | async-done | bytes 4194320 | tf_op jit(solution)/shard_map/all_gather | solution.py:46
  81.0 10.2 %all-to-all-done.1 = f32[32,64,128]{2,0,1:T(8,128)S(1)} async-done(((f32[32,64,128]{2,0,1:T(8,128)}), f32[32,64,128]{2,0,1:T(8,128)S(1)}, u32[]{:S(2)}, u32[]{:S(2)}) %all-to-all-start.1) | async-done | bytes 1048608 | tf_op jit(solution)/shard_map/all_to_all | solution.py:54
  91.2 3.7 %all-to-all-start.3 = ((f32[32,64,128]{2,0,1:T(8,128)}), f32[32,64,128]{2,0,1:T(8,128)S(1)}, u32[]{:S(2)}, u32[]{:S(2)}) async-start(f32[32,64,128]{2,0,1:T(8,128)} %bitcast.76), calls=%async_computation.3 | async-start | bytes 2097152 | tf_op jit(solution)/shard_map/all_to_all | solution.py:60
  99.4 5.8 %fusion.17 = f32[1,1024]{1,0:T(1,128)S(1)} fusion(f32[1024,1]{0,1:T(1,128)S(1)} %bitcast.101, f32[1024,1024]{1,0:T(8,128)} %all-gather.2.cloned.1.call-done), kind=kOutput, calls=%fused_computation.32 | convolution fusion | flops 12582912 | bytes 4202496 | tf_op jit(solution)/shard_map/dot_general | solution.py:36
  105.3 2.4 %fusion.4 = f32[1024,1024]{0,1:T(8,128)} fusion(f32[1024,1024]{1,0:T(8,128)S(1)} %copy-done, f32[1024]{0:T(1024)S(1)} %bitcast.97, f32[1024]{0:T(1024)S(1)} %broadcast_multiply_fusion), kind=kLoop, calls=%fused_computation.5 | loop fusion | flops 2097152 | bytes 8396800 | tf_op jit(solution)/shard_map/dot_general | solution.py:77
  107.6 5.4 %copy.60 = f32[1024,1024]{1,0:T(8,128)} copy(f32[1024,1024]{0,1:T(8,128)} %fusion.4) | data formatting | bytes 8388608 | tf_op jit(solution)/shard_map/dot_general | solution.py:77
  113.0 6.6 %fusion.18 = f32[32,32,256]{2,1,0:T(8,128)} fusion(f32[32,32,1024]{2,1,0:T(8,128)} %bitcast.85, f32[1024,256,1]{1,0,2:T(8,128)S(1)} %bitcast.92), kind=kOutput, calls=%fused_computation.33 | convolution fusion | flops 3221225472 | bytes 6291456 | tf_op jit(solution)/shard_map/dot_general | solution.py:77
  119.6 2.3 %all-to-all-done.3 = f32[32,64,128]{2,0,1:T(8,128)S(1)} async-done(((f32[32,64,128]{2,0,1:T(8,128)}), f32[32,64,128]{2,0,1:T(8,128)S(1)}, u32[]{:S(2)}, u32[]{:S(2)}) %all-to-all-start.3) | async-done | bytes 1048608 | tf_op jit(solution)/shard_map/all_to_all | solution.py:60
  121.9 5.0 %all-to-all-start.6 = ((f32[32,32,256]{2,1,0:T(8,128)}), f32[32,32,256]{2,1,0:T(8,128)S(1)}, u32[]{:S(2)}, u32[]{:S(2)}) async-start(f32[32,32,256]{2,1,0:T(8,128)} %fusion.18), calls=%async_computation.6 | async-start | bytes 2097152 | tf_op jit(solution)/shard_map/all_to_all | solution.py:78
  128.5 2.4 %all_to_all.81 = f32[32,8,1024]{2,0,1:T(8,128)} reshape(f32[32,8,8,128]{3,2,0,1:T(8,128)} %bitcast.90) | data formatting | bytes 2097152 | tf_op jit(solution)/shard_map/all_to_all | solution.py:54
  130.8 6.4 %fusion.9 = f32[32,8,1024]{2,0,1:T(8,128)S(1)} fusion(f32[32,8,1024]{2,0,1:T(8,128)} %all_to_all.81, f32[1024,1024]{1,0:T(8,128)} %all-gather.2.cloned.1.call-done, f32[1024]{0:T(1024)S(1)} %bitcast.98, f32[1024]{0:T(1024)S(1)} %broadcast_multiply_fusion), kind=kOutput, calls=%fused_computation.10 | convolution fusion | flops 3223322624 | bytes 6299648 | tf_op jit(solution)/shard_map/rbk,kj->rbj/dot_general | solution.py:52
  137.2 2.7 %copy.54 = f32[32,8,1024]{0,1,2:T(8,128)} copy(f32[32,8,1024]{2,0,1:T(8,128)S(1)} %fusion.9) | data formatting | bytes 2097152 | tf_op jit(solution)/shard_map/rbk,kj->rbj/dot_general | solution.py:52
  140.0 4.8 %reshape.143 = f32[8,1,32768]{2,1,0:T(1,128)} reshape(f32[1024,8,32]{2,1,0:T(8,128)} %bitcast.81) | data formatting | bytes 2097152
  145.8 4.3 %all-to-all-start.2 = ((f32[8,1,32768]{2,1,0:T(1,128)}), f32[8,1,32768]{2,1,0:T(1,128)S(1)}, u32[]{:S(2)}, u32[]{:S(2)}) async-start(f32[8,1,32768]{2,1,0:T(1,128)} %reshape.143), calls=%async_computation.2 | async-start | bytes 2097152 | tf_op jit(solution)/shard_map/all_to_all | solution.py:64
  151.8 6.4 %fusion.12 = f32[32,8,1024]{2,0,1:T(8,128)S(1)} fusion(f32[32,8,1024]{2,0,1:T(8,128)} %all_to_all.88, f32[1024,1024]{1,0:T(8,128)} %all-gather.2.cloned.1.call-done, f32[1024]{0:T(1024)S(1)} %bitcast.99, f32[1024]{0:T(1024)S(1)} %broadcast_multiply_fusion), kind=kOutput, calls=%fused_computation.11 | convolution fusion | flops 3223322624 | bytes 6299648 | tf_op jit(solution)/shard_map/rbk,kj->rbj/dot_general | solution.py:58
  158.2 2.7 %copy.58 = f32[32,8,1024]{0,1,2:T(8,128)} copy(f32[32,8,1024]{2,0,1:T(8,128)S(1)} %fusion.12) | data formatting | bytes 2097152 | tf_op jit(solution)/shard_map/rbk,kj->rbj/dot_general | solution.py:58
  160.9 4.9 %reshape.145 = f32[8,1,32768]{2,1,0:T(1,128)} reshape(f32[1024,8,32]{2,1,0:T(8,128)} %bitcast.82) | data formatting | bytes 2097152
  165.9 13.5 %all-to-all-done.2 = f32[8,1,32768]{2,1,0:T(1,128)S(1)} async-done(((f32[8,1,32768]{2,1,0:T(1,128)}), f32[8,1,32768]{2,1,0:T(1,128)S(1)}, u32[]{:S(2)}, u32[]{:S(2)}) %all-to-all-start.2) | async-done | bytes 1048608 | tf_op jit(solution)/shard_map/all_to_all | solution.py:64
  179.3 4.2 %all-to-all-start.4 = ((f32[8,1,32768]{2,1,0:T(1,128)}), f32[8,1,32768]{2,1,0:T(1,128)}, u32[]{:S(2)}, u32[]{:S(2)}) async-start(f32[8,1,32768]{2,1,0:T(1,128)} %reshape.145), calls=%async_computation.4 | async-start | bytes 2097152 | tf_op jit(solution)/shard_map/all_to_all | solution.py:65
  189.0 3.1 %reduce.4 = f32[8,32768]{1,0:T(8,128)S(1)} reduce(f32[8,1,32768]{2,1,0:T(1,128)S(1)} %all-to-all-done.2, f32[]{:T(128)} %broadcast.102), dimensions={1}, to_apply=%all_to_all.82.reduce_sub_computation | reduce | bytes 2097156 | tf_op jit(solution)/shard_map/all_to_all | solution.py:64
  192.0 3.3 %reshape.144 = f32[1024,8,32]{2,1,0:T(8,128)} reshape(f32[8,32768]{1,0:T(8,128)S(1)} %reduce.4) | data formatting | bytes 2097152
  195.3 3.9 %copy.55 = f32[32,8,8,128]{3,2,1,0:T(8,128)} copy(f32[32,8,8,128]{0,2,3,1:T(8,128)} %bitcast.83) | data formatting | bytes 2097152 | tf_op jit(solution)/shard_map/all_to_all | solution.py:64
  199.3 13.5 %all-to-all-done.4 = f32[8,1,32768]{2,1,0:T(1,128)} async-done(((f32[8,1,32768]{2,1,0:T(1,128)}), f32[8,1,32768]{2,1,0:T(1,128)}, u32[]{:S(2)}, u32[]{:S(2)}) %all-to-all-start.4) | async-done | bytes 1048608 | tf_op jit(solution)/shard_map/all_to_all | solution.py:65
  212.8 4.3 %reduce.5 = f32[8,32768]{1,0:T(8,128)S(1)} reduce(f32[8,1,32768]{2,1,0:T(1,128)} %all-to-all-done.4, f32[]{:T(128)} %broadcast.102), dimensions={1}, to_apply=%all_to_all.89.reduce_sub_computation | reduce | bytes 2097156 | tf_op jit(solution)/shard_map/all_to_all | solution.py:65
  217.1 3.3 %reshape.146 = f32[1024,8,32]{2,1,0:T(8,128)} reshape(f32[8,32768]{1,0:T(8,128)S(1)} %reduce.5) | data formatting | bytes 2097152
  220.4 3.2 %copy.59 = f32[32,8,8,128]{3,2,1,0:T(8,128)S(1)} copy(f32[32,8,8,128]{0,2,3,1:T(8,128)} %bitcast.84) | data formatting | bytes 2097152 | tf_op jit(solution)/shard_map/all_to_all | solution.py:65
  (39 shorter events, 18.3 us)
Async XLA Ops:
  7.2 73.1 %all-gather.2.cloned.1.call-start = ((), (), s32[]{:S(2)}) async-start(), calls=%async_computation.7 | async-start | bytes 4325376 | tf_op jit(solution)/shard_map/all_gather | solution.py:46
  30.5 32.2 %copy-start.2 = (f32[32,1,64,128]{3,2,1,0:T(8,128)S(1)}, f32[32,1,64,128]{3,2,1,0:T(8,128)}, u32[]{:S(2)}) copy-start(f32[32,1,64,128]{3,2,1,0:T(8,128)} %param.7) | copy-start | bytes 3145732
  32.0 26.3 %all-to-all-start.5 = ((f32[32,32,256]{2,0,1:T(8,128)}), f32[32,32,256]{2,0,1:T(8,128)S(1)}, u32[]{:S(2)}, u32[]{:S(2)}) async-start(f32[32,32,256]{2,0,1:T(8,128)} %copy.61), calls=%async_computation.5 | async-start | bytes 2097152 | tf_op jit(solution)/shard_map/all_to_all | solution.py:76
  58.4 32.8 %all-to-all-start.1 = ((f32[32,64,128]{2,0,1:T(8,128)}), f32[32,64,128]{2,0,1:T(8,128)S(1)}, u32[]{:S(2)}, u32[]{:S(2)}) async-start(f32[32,64,128]{2,0,1:T(8,128)} %bitcast.78), calls=%async_computation.1 | async-start | bytes 2097152 | tf_op jit(solution)/shard_map/all_to_all | solution.py:54
  91.2 30.7 %all-to-all-start.3 = ((f32[32,64,128]{2,0,1:T(8,128)}), f32[32,64,128]{2,0,1:T(8,128)S(1)}, u32[]{:S(2)}, u32[]{:S(2)}) async-start(f32[32,64,128]{2,0,1:T(8,128)} %bitcast.76), calls=%async_computation.3 | async-start | bytes 2097152 | tf_op jit(solution)/shard_map/all_to_all | solution.py:60
  99.4 5.8 %copy-start = (f32[1024,1024]{1,0:T(8,128)S(1)}, f32[1024,1024]{1,0:T(8,128)}, u32[]{:S(2)}) copy-start(f32[1024,1024]{1,0:T(8,128)} %all-gather.2.cloned.1.call-done) | copy-start | bytes 12582916
  121.9 22.9 %all-to-all-start.6 = ((f32[32,32,256]{2,1,0:T(8,128)}), f32[32,32,256]{2,1,0:T(8,128)S(1)}, u32[]{:S(2)}, u32[]{:S(2)}) async-start(f32[32,32,256]{2,1,0:T(8,128)} %fusion.18), calls=%async_computation.6 | async-start | bytes 2097152 | tf_op jit(solution)/shard_map/all_to_all | solution.py:78
  144.8 1.0 copy-start.4
  145.8 33.6 %all-to-all-start.2 = ((f32[8,1,32768]{2,1,0:T(1,128)}), f32[8,1,32768]{2,1,0:T(1,128)S(1)}, u32[]{:S(2)}, u32[]{:S(2)}) async-start(f32[8,1,32768]{2,1,0:T(1,128)} %reshape.143), calls=%async_computation.2 | async-start | bytes 2097152 | tf_op jit(solution)/shard_map/all_to_all | solution.py:64
  160.9 23.5 %copy-start.5 = (f32[32,32,256]{2,1,0:T(8,128)S(1)}, f32[32,32,256]{2,1,0:T(8,128)}, u32[]{:S(2)}) copy-start(f32[32,32,256]{2,1,0:T(8,128)} %copy-done.4) | copy-start | bytes 3145732
  165.9 21.5 %copy-start.1 = (f32[32,64,1,128]{3,2,1,0:T(1,128)S(1)}, f32[32,64,1,128]{3,2,1,0:T(1,128)}, u32[]{:S(2)}) copy-start(f32[32,64,1,128]{3,2,1,0:T(1,128)} %param.8) | copy-start | bytes 3145732
  179.3 33.5 %all-to-all-start.4 = ((f32[8,1,32768]{2,1,0:T(1,128)}), f32[8,1,32768]{2,1,0:T(1,128)}, u32[]{:S(2)}, u32[]{:S(2)}) async-start(f32[8,1,32768]{2,1,0:T(1,128)} %reshape.145), calls=%async_computation.4 | async-start | bytes 2097152 | tf_op jit(solution)/shard_map/all_to_all | solution.py:65
  217.1 6.5 %copy-start.3 = (f32[32,1,64,128]{3,2,1,0:T(8,128)S(1)}, f32[32,1,64,128]{3,2,1,0:T(8,128)}, u32[]{:S(2)}) copy-start(f32[32,1,64,128]{3,2,1,0:T(8,128)} %param.7) | copy-start | bytes 3145732
Sparse Core Ops, SparseCore 0:
  25.3 54.9 all-gather.1
where the time goes:
time: 233 us; the launch traced here: 232 us
  waiting for transfers between devices  69.7 us (30%)
  local copies, waits for them, and re-layouts  54.5 us (23%)
  starting transfers between devices  30.3 us (13%)
  matrix products  25.2 us (11%)
  between operations  18.2 us (8%)
  other arithmetic  17.4 us (7%)
  blocking collectives  16.6 us (7%)
    unnamed x19, local copies, waits for them, and re-layouts  22.3 us
    all_to_all x1, blocking collectives, from_everyone(): lax.all_to_all(jnp.broadcast_to(x[None], (peers, *x.shape)), axis, 0, 0,...  16.6 us
    all_gather x1, waiting for transfers between devices, body(): lax.all_gather(widened, 'row', axis=0, tiled=True)  16 us
    all_to_all x1, waiting for transfers between devices, body(): lax.all_to_all(flat_strip, 'row', split_axis=1, concat_axis=0, tiled=True)  14.1 us
    all_to_all x1, waiting for transfers between devices, body(): lax.all_to_all(strip_turned, 'col', split_axis=2, concat_axis=1, tiled=True)  13.5 us
    all_to_all x1, waiting for transfers between devices, body(): lax.all_to_all(z_turned, 'col', split_axis=2, concat_axis=1, tiled=True)  13.5 us
    all_to_all x1, waiting for transfers between devices, body(): lax.all_to_all(z_blocks, 'col', split_axis=1, concat_axis=2, tiled=True)  10.2 us
    all_to_all x1, starting transfers between devices, body(): lax.all_to_all(flat_strip, 'row', split_axis=1, concat_axis=0, tiled=True)  9.38 us
  transfers between devices with their start and end apart: 7, of which 6 were waited for; matrix products, arithmetic and copies ran while one was open for 34% of the time, Pallas kernels for 0%

commit v1 on v0

--- a/solution.py
+++ b/solution.py
@@ -4,6 +4,11 @@
 from jax.sharding import PartitionSpec as P
 
 W = 1024
+
+
+def gather_over(shard, name, dim):
+    sent = jnp.stack([shard] * lax.axis_size(name))
+    return jnp.concatenate(lax.all_to_all(sent, name, 0, 0), axis=dim)
 
 
 def from_everyone(x, axis):
@@ -43,7 +48,7 @@
     column_position = lax.axis_index("col")
     start_row = window_start[0]
     widened = gather_directly(factor, "col", 1)
-    rotation = reflect(lax.all_gather(widened, "row", axis=0, tiled=True), deflated)
+    rotation = reflect(gather_over(widened, "row", 0), deflated)
     rounds = vectors_window.shape[0]
     blocks = vectors_window.shape[2]
     local_width = vectors_window.shape[3]

time: 233 us -> 279 us (1.20)
  waiting for transfers between devices: 69.7 us -> 119 us
  starting transfers between devices: 30.3 us -> 50.3 us
  blocking collectives: 16.6 us -> 0 us
  between operations: 18.2 us -> 4.68 us
  other arithmetic: 17.4 us -> 23.2 us
  local copies, waits for them, and re-layouts: 54.5 us -> 59 us
  matrix products: 25.2 us -> 22 us
    all_to_all x0 -> x2, waiting for transfers between devices: none -> 50 us  [the longest x1 49.1 us: gather_over(): return jnp.concatenate(lax.all_to_all(sent, name, 0, 0), axis=dim)]
    all_to_all x1, waiting for transfers between devices: 10.2 us -> 29.2 us  [body(): lax.all_to_all(z_blocks, 'col', split_axis=1, concat_axis=2, tiled=True)]
    all_to_all x1 -> x0, blocking collectives: 16.6 us -> none  [from_everyone(): lax.all_to_all(jnp.broadcast_to(x[None], (peers, *x.shape)), axis, 0, 0,...]
    all_gather x1 -> x0, waiting for transfers between devices: 16 us -> none  [body(): lax.all_gather(widened, 'row', axis=0, tiled=True)]
    all_to_all x0 -> x2, starting transfers between devices: none -> 14.1 us  [the longest x1 9 us: from_everyone(): lax.all_to_all(jnp.broadcast_to(x[None], (peers, *x.shape)), axis, 0, 0,...]
    unnamed x19 -> x21, local copies, waits for them, and re-layouts: 22.3 us -> 24.3 us
  transfers between devices with their start and end apart: 7 -> 8, of which waited for: 6 -> 6; matrix products, arithmetic and copies ran while one was open for 34% -> 29% of each run, Pallas kernels for 0% -> 0%
where the time goes in v1:
time: 279 us; the launch traced here: 278 us
  waiting for transfers between devices  119 us (43%)
  local copies, waits for them, and re-layouts  59 us (21%)
  starting transfers between devices  50.3 us (18%)
  other arithmetic  23.2 us (8%)
  matrix products  22 us (8%)
  between operations  4.68 us (2%)
    all_to_all x1, waiting for transfers between devices, gather_over(): return jnp.concatenate(lax.all_to_all(sent, name, 0, 0), axis=dim)  49.1 us
    all_to_all x1, waiting for transfers between devices, body(): lax.all_to_all(z_blocks, 'col', split_axis=1, concat_axis=2, tiled=True)  29.2 us
    unnamed x21, local copies, waits for them, and re-layouts  24.3 us
    all_to_all x1, waiting for transfers between devices, body(): lax.all_to_all(flat_strip, 'row', split_axis=1, concat_axis=0, tiled=True)  14.2 us
    all_to_all x1, waiting for transfers between devices, body(): lax.all_to_all(z_turned, 'col', split_axis=2, concat_axis=1, tiled=True)  13.9 us
    all_to_all x1, waiting for transfers between devices, body(): lax.all_to_all(strip_turned, 'col', split_axis=2, concat_axis=1, tiled=True)  11.4 us
    all_to_all x1, starting transfers between devices, body(): lax.all_to_all(flat_strip, 'row', split_axis=1, concat_axis=0, tiled=True)  9.38 us
    all_to_all x1, starting transfers between devices, from_everyone(): lax.all_to_all(jnp.broadcast_to(x[None], (peers, *x.shape)), axis, 0, 0,...  9 us
  transfers between devices with their start and end apart: 8, of which 6 were waited for; matrix products, arithmetic and copies ran while one was open for 29% of the time, Pallas kernels for 0%

profile of v1, /device:TPU:1, one launch (start us, length us, event | category | flops | bytes accessed | tf_op | source)
XLA Modules:
  0.0 277.9 jit_solution(11860968942480630681)
XLA Ops:
  2.0 9.0 %all-to-all-start = ((f32[8,32,128]{2,1,0:T(8,128)}), f32[8,32,128]{2,1,0:T(8,128)S(1)}, u32[]{:S(2)}, u32[]{:S(2)}) async-start(f32[8,32,128]{2,1,0:T(8,128)} %broadcast_in_dim.42), calls=%async_computation | async-start | bytes 262144 | tf_op jit(solution)/shard_map/all_to_all | solution.py:16
  11.5 4.4 %reduce.3 = f32[32,64,128]{2,1,0:T(8,128)S(1)} reduce(f32[32,64,1,128]{3,2,1,0:T(1,128)} %param.8, f32[]{:T(128)} %broadcast.118), dimensions={2}, to_apply=%param.8.reduce_sub_computation.3 | reduce | bytes 2097156 | tf_op args[2]
  18.8 9.4 %all-to-all-start.6 = ((f32[32,32,256]{2,0,1:T(8,128)}), f32[32,32,256]{2,0,1:T(8,128)S(1)}, u32[]{:S(2)}, u32[]{:S(2)}) async-start(f32[32,32,256]{2,0,1:T(8,128)} %copy.56), calls=%async_computation.6 | async-start | bytes 2097152 | tf_op jit(solution)/shard_map/all_to_all | solution.py:81
  28.2 2.8 %copy.69 = f32[32,1,64,128]{3,0,2,1:T(8,128)} copy(f32[32,1,64,128]{3,2,1,0:T(8,128)} %param.6) | data formatting | bytes 2097152 | tf_op args[0]
  31.0 14.2 %all-to-all-done.6 = f32[32,32,256]{2,0,1:T(8,128)S(1)} async-done(((f32[32,32,256]{2,0,1:T(8,128)}), f32[32,32,256]{2,0,1:T(8,128)S(1)}, u32[]{:S(2)}, u32[]{:S(2)}) %all-to-all-start.6) | async-done | bytes 1048608 | tf_op jit(solution)/shard_map/all_to_all | solution.py:81
  45.2 4.7 %all-to-all-start.2 = ((f32[32,64,128]{2,0,1:T(8,128)}), f32[32,64,128]{2,0,1:T(8,128)S(1)}, u32[]{:S(2)}, u32[]{:S(2)}) async-start(f32[32,64,128]{2,0,1:T(8,128)} %bitcast.77), calls=%async_computation.2 | async-start | bytes 2097152 | tf_op jit(solution)/shard_map/all_to_all | solution.py:59
  49.9 29.2 %all-to-all-done.2 = f32[32,64,128]{2,0,1:T(8,128)S(1)} async-done(((f32[32,64,128]{2,0,1:T(8,128)}), f32[32,64,128]{2,0,1:T(8,128)S(1)}, u32[]{:S(2)}, u32[]{:S(2)}) %all-to-all-start.2) | async-done | bytes 1048608 | tf_op jit(solution)/shard_map/all_to_all | solution.py:59
  81.6 5.0 %all-to-all-start.1 = ((f32[32,32,1024]{2,1,0:T(8,128)}), f32[32,32,1024]{2,1,0:T(8,128)}, u32[]{:S(2)}, u32[]{:S(2)}) async-start(f32[32,32,1024]{2,1,0:T(8,128)} %stack.3), calls=%async_computation.1 | async-start | bytes 8388608 | tf_op jit(solution)/shard_map/all_to_all | solution.py:11
  88.3 49.1 %all-to-all-done.1 = f32[32,32,1024]{2,1,0:T(8,128)} async-done(((f32[32,32,1024]{2,1,0:T(8,128)}), f32[32,32,1024]{2,1,0:T(8,128)}, u32[]{:S(2)}, u32[]{:S(2)}) %all-to-all-start.1) | async-done | bytes 4194336 | tf_op jit(solution)/shard_map/all_to_all | solution.py:11
  137.4 3.7 %all-to-all-start.4 = ((f32[32,64,128]{2,0,1:T(8,128)}), f32[32,64,128]{2,0,1:T(8,128)S(1)}, u32[]{:S(2)}, u32[]{:S(2)}) async-start(f32[32,64,128]{2,0,1:T(8,128)} %bitcast.75), calls=%async_computation.4 | async-start | bytes 2097152 | tf_op jit(solution)/shard_map/all_to_all | solution.py:65
  147.6 5.6 %fusion.1 = f32[1,1024]{1,0:T(1,128)S(1)} fusion(f32[1024,1024]{1,0:T(8,128)} %bitcast.2, f32[1,1024]{1,0:T(1,128)S(1)} %fusion), kind=kOutput, calls=%fused_computation.16 | convolution fusion | flops 12582912 | bytes 4202496 | tf_op jit(solution)/shard_map/dot_general | solution.py:41
  153.3 4.6 %subtract_bitcast_fusion = f32[1024,1024]{0,1:T(8,128)} fusion(f32[1024]{0:T(1024)S(1)} %bitcast.96, f32[1024]{0:T(1024)S(1)} %broadcast_multiply_fusion, f32[32,32,1024]{2,1,0:T(8,128)} %all-to-all-done.1), kind=kLoop, calls=%fused_computation | loop fusion | flops 2097152 | bytes 8396800 | tf_op jit(solution)/shard_map/dot_general | solution.py:82
  157.9 5.4 %copy.55 = f32[1024,1024]{1,0:T(8,128)} copy(f32[1024,1024]{0,1:T(8,128)} %subtract_bitcast_fusion) | data formatting | bytes 8388608 | tf_op jit(solution)/shard_map/dot_general | solution.py:82
  163.2 6.6 %fusion.3 = f32[32,32,256]{2,1,0:T(8,128)} fusion(f32[32,32,1024]{2,1,0:T(8,128)} %bitcast.84, f32[1024,256,1]{1,0,2:T(8,128)S(1)} %bitcast.93), kind=kOutput, calls=%fused_computation.23 | convolution fusion | flops 3221225472 | bytes 6291456 | tf_op jit(solution)/shard_map/dot_general | solution.py:82
  169.8 7.3 %all-to-all-start.7 = ((f32[32,32,256]{2,1,0:T(8,128)}), f32[32,32,256]{2,1,0:T(8,128)S(1)}, u32[]{:S(2)}, u32[]{:S(2)}) async-start(f32[32,32,256]{2,1,0:T(8,128)} %fusion.3), calls=%async_computation.7 | async-start | bytes 2097152 | tf_op jit(solution)/shard_map/all_to_all | solution.py:83
  181.1 2.7 multiply_subtract_fusion
  185.7 3.8 %convolution_bitcast_fusion.1 = f32[32,8,1024]{2,0,1:T(8,128)S(1)} fusion(f32[1024,1024,1]{1,0,2:T(8,128)S(1)} %bitcast.91, f32[32,8,1024]{2,0,1:T(8,128)S(1)} %copy-done.6), kind=kOutput, calls=%fused_computation.3 | convolution fusion | flops 3221225472 | bytes 6291456 | tf_op jit(solution)/shard_map/rbk,kj->rbj/dot_general | solution.py:57
  189.6 2.7 copy.49
  192.3 4.8 %reshape.168 = f32[8,1,32768]{2,1,0:T(1,128)} reshape(f32[1024,8,32]{2,1,0:T(8,128)} %bitcast.80) | data formatting | bytes 2097152
  198.1 6.7 %all-to-all-start.3 = ((f32[8,1,32768]{2,1,0:T(1,128)}), f32[8,1,32768]{2,1,0:T(1,128)S(1)}, u32[]{:S(2)}, u32[]{:S(2)}) async-start(f32[8,1,32768]{2,1,0:T(1,128)} %reshape.168), calls=%async_computation.3 | async-start | bytes 2097152 | tf_op jit(solution)/shard_map/all_to_all | solution.py:69
  206.5 6.0 %convolution_bitcast_fusion = f32[32,8,1024]{2,0,1:T(8,128)S(1)} fusion(f32[1024,1024,1]{1,0,2:T(8,128)} %bitcast.92, f32[32,8,1024]{2,0,1:T(8,128)} %all_to_all.92), kind=kOutput, calls=%fused_computation.2 | convolution fusion | flops 3221225472 | bytes 6291456 | tf_op jit(solution)/shard_map/rbk,kj->rbj/dot_general | solution.py:63
  212.5 2.7 copy.53
  215.2 4.9 %reshape.170 = f32[8,1,32768]{2,1,0:T(1,128)} reshape(f32[1024,8,32]{2,1,0:T(8,128)} %bitcast.81) | data formatting | bytes 2097152
  220.1 13.9 %all-to-all-done.3 = f32[8,1,32768]{2,1,0:T(1,128)S(1)} async-done(((f32[8,1,32768]{2,1,0:T(1,128)}), f32[8,1,32768]{2,1,0:T(1,128)S(1)}, u32[]{:S(2)}, u32[]{:S(2)}) %all-to-all-start.3) | async-done | bytes 1048608 | tf_op jit(solution)/shard_map/all_to_all | solution.py:69
  234.0 4.5 %all-to-all-start.5 = ((f32[8,1,32768]{2,1,0:T(1,128)}), f32[8,1,32768]{2,1,0:T(1,128)}, u32[]{:S(2)}, u32[]{:S(2)}) async-start(f32[8,1,32768]{2,1,0:T(1,128)} %reshape.170), calls=%async_computation.5 | async-start | bytes 2097152 | tf_op jit(solution)/shard_map/all_to_all | solution.py:70
  244.0 3.1 %reduce.4 = f32[8,32768]{1,0:T(8,128)S(1)} reduce(f32[8,1,32768]{2,1,0:T(1,128)S(1)} %all-to-all-done.3, f32[]{:T(128)} %broadcast.119), dimensions={1}, to_apply=%all_to_all.86.reduce_sub_computation | reduce | bytes 2097156 | tf_op jit(solution)/shard_map/all_to_all | solution.py:69
  247.1 3.3 %reshape.169 = f32[1024,8,32]{2,1,0:T(8,128)} reshape(f32[8,32768]{1,0:T(8,128)S(1)} %reduce.4) | data formatting | bytes 2097152
  250.4 3.9 %copy.50 = f32[32,8,8,128]{3,2,1,0:T(8,128)} copy(f32[32,8,8,128]{0,2,3,1:T(8,128)} %bitcast.82) | data formatting | bytes 2097152 | tf_op jit(solution)/shard_map/all_to_all | solution.py:69
  254.3 11.4 %all-to-all-done.5 = f32[8,1,32768]{2,1,0:T(1,128)} async-done(((f32[8,1,32768]{2,1,0:T(1,128)}), f32[8,1,32768]{2,1,0:T(1,128)}, u32[]{:S(2)}, u32[]{:S(2)}) %all-to-all-start.5) | async-done | bytes 1048608 | tf_op jit(solution)/shard_map/all_to_all | solution.py:70
  265.7 4.4 %reduce.5 = f32[8,32768]{1,0:T(8,128)S(1)} reduce(f32[8,1,32768]{2,1,0:T(1,128)} %all-to-all-done.5, f32[]{:T(128)} %broadcast.119), dimensions={1}, to_apply=%all_to_all.93.reduce_sub_computation | reduce | bytes 2097156 | tf_op jit(solution)/shard_map/all_to_all | solution.py:70
  270.1 3.3 %reshape.171 = f32[1024,8,32]{2,1,0:T(8,128)} reshape(f32[8,32768]{1,0:T(8,128)S(1)} %reduce.5) | data formatting | bytes 2097152
  273.4 3.2 %copy.54 = f32[32,8,8,128]{3,2,1,0:T(8,128)S(1)} copy(f32[32,8,8,128]{0,2,3,1:T(8,128)} %bitcast.83) | data formatting | bytes 2097152 | tf_op jit(solution)/shard_map/all_to_all | solution.py:70
  (43 shorter events, 26.8 us)
Async XLA Ops:
  2.0 16.8 %all-to-all-start = ((f32[8,32,128]{2,1,0:T(8,128)}), f32[8,32,128]{2,1,0:T(8,128)S(1)}, u32[]{:S(2)}, u32[]{:S(2)}) async-start(f32[8,32,128]{2,1,0:T(8,128)} %broadcast_in_dim.42), calls=%async_computation | async-start | bytes 262144 | tf_op jit(solution)/shard_map/all_to_all | solution.py:16
  18.8 26.4 %all-to-all-start.6 = ((f32[32,32,256]{2,0,1:T(8,128)}), f32[32,32,256]{2,0,1:T(8,128)S(1)}, u32[]{:S(2)}, u32[]{:S(2)}) async-start(f32[32,32,256]{2,0,1:T(8,128)} %copy.56), calls=%async_computation.6 | async-start | bytes 2097152 | tf_op jit(solution)/shard_map/all_to_all | solution.py:81
  45.2 33.9 %all-to-all-start.2 = ((f32[32,64,128]{2,0,1:T(8,128)}), f32[32,64,128]{2,0,1:T(8,128)S(1)}, u32[]{:S(2)}, u32[]{:S(2)}) async-start(f32[32,64,128]{2,0,1:T(8,128)} %bitcast.77), calls=%async_computation.2 | async-start | bytes 2097152 | tf_op jit(solution)/shard_map/all_to_all | solution.py:59
  81.6 5.1 %copy-start.1 = (f32[32,1,64,128]{3,2,1,0:T(8,128)S(1)}, f32[32,1,64,128]{3,2,1,0:T(8,128)}, u32[]{:S(2)}) copy-start(f32[32,1,64,128]{3,2,1,0:T(8,128)} %param.7) | copy-start | bytes 3145732
  81.6 55.8 %all-to-all-start.1 = ((f32[32,32,1024]{2,1,0:T(8,128)}), f32[32,32,1024]{2,1,0:T(8,128)}, u32[]{:S(2)}, u32[]{:S(2)}) async-start(f32[32,32,1024]{2,1,0:T(8,128)} %stack.3), calls=%async_computation.1 | async-start | bytes 8388608 | tf_op jit(solution)/shard_map/all_to_all | solution.py:11
  137.4 32.4 %all-to-all-start.4 = ((f32[32,64,128]{2,0,1:T(8,128)}), f32[32,64,128]{2,0,1:T(8,128)S(1)}, u32[]{:S(2)}, u32[]{:S(2)}) async-start(f32[32,64,128]{2,0,1:T(8,128)} %bitcast.75), calls=%async_computation.4 | async-start | bytes 2097152 | tf_op jit(solution)/shard_map/all_to_all | solution.py:65
  169.8 27.3 %all-to-all-start.7 = ((f32[32,32,256]{2,1,0:T(8,128)}), f32[32,32,256]{2,1,0:T(8,128)S(1)}, u32[]{:S(2)}, u32[]{:S(2)}) async-start(f32[32,32,256]{2,1,0:T(8,128)} %fusion.3), calls=%async_computation.7 | async-start | bytes 2097152 | tf_op jit(solution)/shard_map/all_to_all | solution.py:83
  181.1 4.6 %copy-start.6 = (f32[32,8,1024]{2,0,1:T(8,128)S(1)}, f32[32,8,1024]{2,0,1:T(8,128)}, u32[]{:S(2)}) copy-start(f32[32,8,1024]{2,0,1:T(8,128)} %all_to_all.85) | copy-start | bytes 3145732
  183.8 2.0 copy-start.5
  197.1 1.0 copy-start.3
  198.1 35.9 %all-to-all-start.3 = ((f32[8,1,32768]{2,1,0:T(1,128)}), f32[8,1,32768]{2,1,0:T(1,128)S(1)}, u32[]{:S(2)}, u32[]{:S(2)}) async-start(f32[8,1,32768]{2,1,0:T(1,128)} %reshape.168), calls=%async_computation.3 | async-start | bytes 2097152 | tf_op jit(solution)/shard_map/all_to_all | solution.py:69
  215.2 24.1 %copy-start.4 = (f32[32,32,256]{2,1,0:T(8,128)S(1)}, f32[32,32,256]{2,1,0:T(8,128)}, u32[]{:S(2)}) copy-start(f32[32,32,256]{2,1,0:T(8,128)} %copy-done.3) | copy-start | bytes 3145732
  220.1 22.1 %copy-start = (f32[32,64,1,128]{3,2,1,0:T(1,128)S(1)}, f32[32,64,1,128]{3,2,1,0:T(1,128)}, u32[]{:S(2)}) copy-start(f32[32,64,1,128]{3,2,1,0:T(1,128)} %param.8) | copy-start | bytes 3145732
  234.0 31.7 %all-to-all-start.5 = ((f32[8,1,32768]{2,1,0:T(1,128)}), f32[8,1,32768]{2,1,0:T(1,128)}, u32[]{:S(2)}, u32[]{:S(2)}) async-start(f32[8,1,32768]{2,1,0:T(1,128)} %reshape.170), calls=%async_computation.5 | async-start | bytes 2097152 | tf_op jit(solution)/shard_map/all_to_all | solution.py:70
  270.1 6.6 %copy-start.2 = (f32[32,1,64,128]{3,2,1,0:T(8,128)S(1)}, f32[32,1,64,128]{3,2,1,0:T(8,128)}, u32[]{:S(2)}) copy-start(f32[32,1,64,128]{3,2,1,0:T(8,128)} %param.7) | copy-start | bytes 3145732
